TPU v7x, 32 devices: a whole 2x2x4 slice. The times are simulated.
32 devices in a mesh: pz: 4 (over z), py: 8 (over y, x, core).
Axes of the slice: x: 2, y: 2, z: 4, core: 2. Of those that a mesh axis runs over, the one named last changes fastest.
Arguments:
- populations: float32 [19, 256, 64, 256], P(None, None, 'py', 'pz')
- relax_time: float32 [], replicated
- body_force: float32 [3], replicated
Outputs:
- output 1: float32 [19, 256, 64, 256], P(None, None, 'py', 'pz')
- output 2: float32 [256, 64, 256], P(None, 'py', 'pz')
- output 3: float32 [3, 256, 64, 256], P(None, None, 'py', 'pz')
All inputs are finite; a program needn't handle non-finite values.
Results may differ from a plain program's by a relative error of at most 0.001.
Values sent between devices are 32-bit elements.
A program may use at most 1 GiB of HBM per device.

v0:
```python
import functools

import jax
import jax.numpy as jnp
from jax import lax
from jax.experimental import pallas as pl
from jax.experimental.pallas import tpu as pltpu
from jax.sharding import PartitionSpec as P

STEPS = 4
VELOCITIES = ((0, 0, 0), (1, 0, 0), (-1, 0, 0), (0, 1, 0), (0, -1, 0), (0, 0, 1), (0, 0, -1), (1, 1, 0), (-1, -1, 0), (1, -1, 0), (-1, 1, 0), (1, 0, 1), (-1, 0, -1), (1, 0, -1), (-1, 0, 1), (0, 1, 1), (0, -1, -1), (0, 1, -1), (0, -1, 1))
ORDER = (17, 3, 7, 10, 15, 5, 11, 14, 18, 4, 8, 9, 16, 6, 12, 13, 0, 1, 2)
SLOT = {pop_id: slot for slot, pop_id in enumerate(ORDER)}
MESH = pl.DeviceIdType.MESH
LANES = 128
ROWS = 8
COPIES = 16


def moment_sums(load):
    rest = load(0)
    total = rest
    diff = {}
    for plus in range(1, 19, 2):
        upper, lower = load(plus), load(plus + 1)
        total = total + (upper + lower)
        diff[plus] = upper - lower
    mom_x = (diff[1] + diff[7]) + (diff[9] + (diff[11] + diff[13]))
    mom_y = (diff[3] + diff[7]) - (diff[9] - (diff[15] + diff[17]))
    mom_z = (diff[5] + diff[11]) - (diff[13] - (diff[15] - diff[17]))
    return total, (mom_x, mom_y, mom_z)


def tile_terms(load, force, rate36):
    density, momentum = moment_sums(load)
    inverse = 1.0 / density
    half = [(momentum[axis] + force[axis]) * inverse * 1.5 for axis in range(3)]
    square = half[0] * half[0] + half[1] * half[1] + half[2] * half[2]
    scale = density * rate36
    even = scale * (1.0 - square * (2.0 / 3.0))
    twice = scale + scale
    odd = [twice * half[axis] for axis in range(3)]
    return even, odd, half


def relaxed(load, terms, keep, plus):
    even, odd, half = terms
    axes = [(axis, shift) for axis, shift in enumerate(VELOCITIES[plus]) if shift != 0]
    if len(axes) == 1:
        axis = axes[0][0]
        odd_part = odd[axis] + odd[axis]
        even_part = (even + even) + odd_part * half[axis]
    else:
        (first, _), (second, sign) = axes
        if sign > 0:
            odd_part = odd[first] + odd[second]
            projection = half[first] + half[second]
        else:
            odd_part = odd[first] - odd[second]
            projection = half[first] - half[second]
        even_part = even + odd_part * projection
    return load(plus) * keep + (even_part + odd_part), load(plus + 1) * keep + (even_part - odd_part)


def rolled(halves, shift, lane):
    if shift == 0:
        return halves
    moved = [pltpu.roll(part, shift % LANES, 1) for part in halves]
    edge = lane == (0 if shift > 0 else LANES - 1)
    return [jnp.where(edge, moved[1], moved[0]), jnp.where(edge, moved[0], moved[1])]


def step_kernel(size_y, size_z, ny, nz, tau_ref, force_ref, field_ref, out_ref, stage, other, load_sem, send_sem, recv_sem):
    me_y, me_z = lax.axis_index("py"), lax.axis_index("pz")
    up_y, down_y = lax.rem(me_y + 1, size_y), lax.rem(me_y + size_y - 1, size_y)
    up_z, down_z = lax.rem(me_z + 1, size_z), lax.rem(me_z + size_z - 1, size_z)

    def device(dev_y, dev_z):
        return {"py": dev_y, "pz": dev_z}

    barrier = pltpu.get_barrier_semaphore()
    neighbours = [device(dy, dz) for dy in (down_y, me_y, up_y) for dz in (down_z, me_z, up_z)]
    del neighbours[4]
    for neighbour in neighbours:
        pl.semaphore_signal(barrier, inc=1, device_id=neighbour, device_id_type=MESH)

    plane_order = [0, ny - 1] + list(range(1, ny - 1))
    loads = {y: pltpu.make_async_copy(field_ref.at[:, y], stage.at[:, y], load_sem.at[y]) for y in plane_order}
    for y in plane_order:
        loads[y].start()

    tau = jnp.full((ROWS, LANES), tau_ref[0], jnp.float32)
    rate = 1.0 / tau
    keep = 1.0 - rate
    rate36 = rate * (1.0 / 36.0)
    force = [tau * force_ref[axis] for axis in range(3)]
    lane = lax.broadcasted_iota(jnp.int32, (ROWS, LANES), 1)
    first_row, last_row = ROWS, ROWS + nz - 1
    buffers = (other, out_ref)
    tiles = nz // ROWS

    def collide_tile(step, y, tile):
        row = pl.multiple_of(tile * ROWS, ROWS)
        target = buffers[step % 2]
        source = buffers[(step + 1) % 2]

        def load(half, pop_id):
            if step == 0:
                return stage[pop_id, y, pl.ds(row, ROWS), pl.ds(half * LANES, LANES)]
            return source[SLOT[pop_id], y + 1 - VELOCITIES[pop_id][1], half, pl.ds(row + ROWS, ROWS), :]

        def store(pop_id, halves):
            shift_x, _, shift_z = VELOCITIES[pop_id]
            halves = rolled(halves, shift_x, lane)
            for half in range(2):
                target[SLOT[pop_id], y + 1, half, pl.ds(row + (ROWS + shift_z), ROWS), :] = halves[half]

        loaders = [functools.partial(load, half) for half in range(2)]
        terms = [tile_terms(loaders[half], force, rate36) for half in range(2)]
        store(0, [loaders[half](0) * keep + terms[half][0] * 12.0 for half in range(2)])
        for plus in range(1, 19, 2):
            pairs = [relaxed(loaders[half], terms[half], keep, plus) for half in range(2)]
            store(plus, [pair[0] for pair in pairs])
            store(plus + 1, [pair[1] for pair in pairs])

    def copies(step):
        state = buffers[step % 2]
        parity = step % 2
        result = []

        def add(source, target, dev_y, dev_z):
            number = len(result)
            result.append(pltpu.make_async_remote_copy(
                src_ref=source, dst_ref=target, send_sem=send_sem.at[parity, number], recv_sem=recv_sem.at[parity, number],
                device_id=device(dev_y, dev_z), device_id_type=MESH))

        inner = pl.ds(first_row, nz)
        without_first, without_last = pl.ds(first_row + 1, nz - 1), pl.ds(first_row, nz - 1)
        for slots, rows in ((pl.ds(1, 3), inner), (pl.ds(4, 1), without_first), (pl.ds(0, 1), without_last)):
            add(state.at[slots, ny, :, rows, :], state.at[slots, 0, :, rows, :], up_y, me_z)
        for slots, rows in ((pl.ds(9, 3), inner), (pl.ds(8, 1), without_first), (pl.ds(12, 1), without_last)):
            add(state.at[slots, 1, :, rows, :], state.at[slots, ny + 1, :, rows, :], down_y, me_z)
        all_planes, lower_planes, upper_planes = pl.ds(1, ny), pl.ds(1, ny - 1), pl.ds(2, ny - 1)
        out_up, out_down = pl.ds(last_row + 1, 1), pl.ds(first_row - 1, 1)
        in_up, in_down = pl.ds(first_row, 1), pl.ds(last_row, 1)
        for slots, planes in ((pl.ds(5, 3), all_planes), (pl.ds(4, 1), lower_planes), (pl.ds(8, 1), upper_planes)):
            add(state.at[slots, planes, :, out_up, :], state.at[slots, planes, :, in_up, :], me_y, up_z)
        for slots, planes in ((pl.ds(13, 3), all_planes), (pl.ds(0, 1), lower_planes), (pl.ds(12, 1), upper_planes)):
            add(state.at[slots, planes, :, out_down, :], state.at[slots, planes, :, in_down, :], me_y, down_z)
        add(state.at[4, ny, :, out_up, :], state.at[4, 0, :, in_up, :], up_y, up_z)
        add(state.at[0, ny, :, out_down, :], state.at[0, 0, :, in_down, :], up_y, down_z)
        add(state.at[8, 1, :, out_up, :], state.at[8, ny + 1, :, in_up, :], down_y, up_z)
        add(state.at[12, 1, :, out_down, :], state.at[12, ny + 1, :, in_down, :], down_y, down_z)
        return result

    def over(count, body):
        def run(index, carry):
            body(index)
            return carry
        lax.fori_loop(0, count, run, 0)

    started = [copies(step) for step in range(STEPS)]
    for step in range(STEPS):
        if step == 0:
            loads[0].wait()
            loads[ny - 1].wait()
        else:
            for copy in started[step - 1]:
                copy.wait_recv()
        if step >= 2:
            for copy in started[step - 2]:
                copy.wait_send()
        over(2 * tiles, lambda index: collide_tile(step, (index // tiles) * (ny - 1), index % tiles))
        if step == 0:
            pl.semaphore_wait(barrier, len(neighbours))
        for copy in started[step][:6]:
            copy.start()
        if step == 0:
            for y in range(1, ny - 1):
                loads[y].wait()
        over(2 * (ny - 2), lambda index: collide_tile(step, 1 + index // 2, (index % 2) * (tiles - 1)))
        for copy in started[step][6:]:
            copy.start()
        over((ny - 2) * (tiles - 2), lambda index: collide_tile(step, 1 + index // (tiles - 2), 1 + index % (tiles - 2)))
    for copy in started[STEPS - 1]:
        copy.wait_recv()
    for step in (STEPS - 2, STEPS - 1):
        for copy in started[step]:
            copy.wait_send()


def output_kernel(ny, nz, tau_ref, force_ref, state, field_ref, density_ref, velocity_ref, moments, field_sem, moment_sem):
    field_copies = []
    for pop_id in range(19):
        shift_y = VELOCITIES[pop_id][1]
        for half in range(2):
            field_copies.append(pltpu.make_async_copy(
                state.at[SLOT[pop_id], pl.ds(1 - shift_y, ny), half, pl.ds(ROWS, nz), :],
                field_ref.at[pop_id, :, :, pl.ds(half * LANES, LANES)], field_sem.at[2 * pop_id + half]))
    for copy in field_copies:
        copy.start()
    tau = jnp.full((ROWS, LANES), tau_ref[0], jnp.float32)
    force = [tau * force_ref[axis] for axis in range(3)]
    tiles = nz // ROWS
    moment_copies = []
    for y in range(ny):
        def tile_moments(tile, carry):
            row = pl.multiple_of(tile * ROWS, ROWS)
            for half in range(2):
                def load(pop_id):
                    return state[SLOT[pop_id], y + 1 - VELOCITIES[pop_id][1], half, pl.ds(row + ROWS, ROWS), :]
                density, momentum = moment_sums(load)
                inverse = 1.0 / density
                place = (y, pl.ds(row, ROWS), pl.ds(half * LANES, LANES))
                moments[(0, *place)] = density
                for axis in range(3):
                    moments[(1 + axis, *place)] = (momentum[axis] + force[axis]) * inverse
            return carry
        lax.fori_loop(0, tiles, tile_moments, 0)
        moment_copies.append(pltpu.make_async_copy(moments.at[0, y], density_ref.at[y], moment_sem.at[0, y]))
        moment_copies.append(pltpu.make_async_copy(moments.at[pl.ds(1, 3), y], velocity_ref.at[:, y], moment_sem.at[1, y]))
        moment_copies[-2].start()
        moment_copies[-1].start()
    for copy in field_copies + moment_copies:
        copy.wait()


def solution(mesh):
    size_y = mesh.shape["py"]
    size_z = mesh.shape["pz"]
    field_spec = P(None, None, "py", "pz")

    def local_steps(populations, relax_time, body_force):
        field = jnp.transpose(populations, (0, 2, 3, 1))
        _, ny, nz, nx = field.shape
        tau = jnp.reshape(relax_time, (1,))
        state_shape = (19, ny + 2, 2, nz + 2 * ROWS, LANES)
        smem = pl.BlockSpec(memory_space=pltpu.SMEM)
        vmem = pl.BlockSpec(memory_space=pltpu.VMEM)
        anywhere = pl.BlockSpec(memory_space=pl.ANY)
        state = pl.pallas_call(
            functools.partial(step_kernel, size_y, size_z, ny, nz),
            name="lattice_steps",
            out_shape=pltpu.VMEM(state_shape, jnp.float32),
            in_specs=[smem, smem, anywhere],
            out_specs=vmem,
            scratch_shapes=[
                pltpu.VMEM((19, ny, nz, nx), jnp.float32),
                pltpu.VMEM(state_shape, jnp.float32),
                pltpu.SemaphoreType.DMA((ny,)),
                pltpu.SemaphoreType.DMA((2, COPIES)),
                pltpu.SemaphoreType.DMA((2, COPIES)),
            ],
            compiler_params=pltpu.CompilerParams(collective_id=0, has_side_effects=True, vmem_limit_bytes=44 * 2**20),
        )(tau, body_force, field)
        final, density, velocity = pl.pallas_call(
            functools.partial(output_kernel, ny, nz),
            name="lattice_output",
            out_shape=(
                jax.ShapeDtypeStruct((19, ny, nz, nx), jnp.float32),
                jax.ShapeDtypeStruct((ny, nz, nx), jnp.float32),
                jax.ShapeDtypeStruct((3, ny, nz, nx), jnp.float32),
            ),
            in_specs=[smem, smem, vmem],
            out_specs=(anywhere, anywhere, anywhere),
            scratch_shapes=[
                pltpu.VMEM((4, ny, nz, nx), jnp.float32),
                pltpu.SemaphoreType.DMA((38,)),
                pltpu.SemaphoreType.DMA((2, ny)),
            ],
            compiler_params=pltpu.CompilerParams(vmem_limit_bytes=24 * 2**20),
        )(tau, body_force, state)
        return jnp.transpose(final, (0, 3, 1, 2)), jnp.transpose(density, (2, 0, 1)), jnp.transpose(velocity, (0, 3, 1, 2))

    return jax.shard_map(local_steps, mesh=mesh, in_specs=(field_spec, P(), P()), out_specs=(field_spec, P(None, "py", "pz"), field_spec), check_vma=False)
```

profile of v0, /device:TPU:0, one launch (start us, length us, event | category | flops | bytes accessed | tf_op | source)
XLA Modules:
  0.0 54.3 jit_solution(4415229642094967122)
XLA Ops:
  1.3 0.0 copy-start
  1.3 47.6 %lattice_steps.1.state = f32[19,10,2,80,128]{4,3,2,1,0:T(8,128)S(1)} custom-call(f32[1]{0:T(128)} %bitcast.5.tau_ref, f32[3]{0:T(128)} %force_ref.3, f32[19,8,64,256]{3,2,1,0:T(8,128)} %bitcast.7), custom_call_target="tpu_custom_call" | custom-call | tf_op jit(solution)/shard_map/lattice_steps/pallas_call | solution.py:241
  48.9 0.0 copy-done
  48.9 5.4 %lattice_output.1 = (f32[19,8,64,256]{3,2,1,0:T(8,128)}, f32[8,64,256]{2,1,0:T(8,128)}, f32[3,8,64,256]{3,2,1,0:T(8,128)}) custom-call(f32[1]{0:T(128)} %bitcast.6.tau_ref, f32[3]{0:T(128)S(1)} %copy-done, f32[19,10,2,80,128]{4,3,2,1,0:T(8,128)S(1)} %lattice_steps.1.state), custom_call_target="tpu_custom_call" | custom-call | tf_op jit(solution)/shard_map/lattice_output/pallas_call | solution.py:256
Async XLA Ops:
  1.3 47.6 %copy-start = (f32[3]{0:T(128)S(1)}, f32[3]{0:T(128)}, u32[]{:S(2)}) copy-start(f32[3]{0:T(128)} %force_ref.3) | copy-start | bytes 40
where the time goes:
time: 54.5 us; the launch traced here: 54.3 us
  Pallas kernels  53 us (97%)
  between operations  1.3 us (2%)
    pallas_call x1, Pallas kernels, local_steps(): pl.pallas_call(functools.partial(step_kernel, size_y, size_z, ny, nz), na...  47.6 us
    pallas_call x1, Pallas kernels, local_steps(): pl.pallas_call(functools.partial(output_kernel, ny, nz), name='lattice_ou...  5.37 us

commit v1 on v0

--- a/solution.py
+++ b/solution.py
@@ -14,7 +14,7 @@
 MESH = pl.DeviceIdType.MESH
 LANES = 128
 ROWS = 8
-COPIES = 16
+EDGE_COPIES = 7
 
 
 def moment_sums(load):
@@ -70,7 +70,7 @@
     return [jnp.where(edge, moved[1], moved[0]), jnp.where(edge, moved[0], moved[1])]
 
 
-def step_kernel(size_y, size_z, ny, nz, tau_ref, force_ref, field_ref, out_ref, stage, other, load_sem, send_sem, recv_sem):
+def step_kernel(size_y, size_z, ny, nz, tau_ref, force_ref, field_ref, out_ref, stage, other, load_sem, face_send, face_recv, edge_send, edge_recv):
     me_y, me_z = lax.axis_index("py"), lax.axis_index("pz")
     up_y, down_y = lax.rem(me_y + 1, size_y), lax.rem(me_y + size_y - 1, size_y)
     up_z, down_z = lax.rem(me_z + 1, size_z), lax.rem(me_z + size_z - 1, size_z)
@@ -95,7 +95,6 @@
     rate36 = rate * (1.0 / 36.0)
     force = [tau * force_ref[axis] for axis in range(3)]
     lane = lax.broadcasted_iota(jnp.int32, (ROWS, LANES), 1)
-    first_row, last_row = ROWS, ROWS + nz - 1
     buffers = (other, out_ref)
     tiles = nz // ROWS
 
@@ -107,13 +106,13 @@
         def load(half, pop_id):
             if step == 0:
                 return stage[pop_id, y, pl.ds(row, ROWS), pl.ds(half * LANES, LANES)]
-            return source[SLOT[pop_id], y + 1 - VELOCITIES[pop_id][1], half, pl.ds(row + ROWS, ROWS), :]
+            _, shift_y, shift_z = VELOCITIES[pop_id]
+            return source[SLOT[pop_id], y + 1 - shift_y, half, pl.ds(row + (ROWS - shift_z), ROWS), :]
 
         def store(pop_id, halves):
-            shift_x, _, shift_z = VELOCITIES[pop_id]
-            halves = rolled(halves, shift_x, lane)
+            halves = rolled(halves, VELOCITIES[pop_id][0], lane)
             for half in range(2):
-                target[SLOT[pop_id], y + 1, half, pl.ds(row + (ROWS + shift_z), ROWS), :] = halves[half]
+                target[SLOT[pop_id], y + 1, half, pl.ds(row + ROWS, ROWS), :] = halves[half]
 
         loaders = [functools.partial(load, half) for half in range(2)]
         terms = [tile_terms(loaders[half], force, rate36) for half in range(2)]
@@ -123,79 +122,124 @@
             store(plus, [pair[0] for pair in pairs])
             store(plus + 1, [pair[1] for pair in pairs])
 
-    def copies(step):
-        state = buffers[step % 2]
-        parity = step % 2
+    def faces(step, tile):
+        state, parity = buffers[step % 2], step % 2
+        rows = pl.ds(pl.multiple_of(tile * ROWS + ROWS, ROWS), ROWS)
         result = []
-
-        def add(source, target, dev_y, dev_z):
-            number = len(result)
+        for face, (slots, source, target, dev_y) in enumerate(((pl.ds(0, 5), ny, 0, up_y), (pl.ds(8, 5), 1, ny + 1, down_y))):
             result.append(pltpu.make_async_remote_copy(
-                src_ref=source, dst_ref=target, send_sem=send_sem.at[parity, number], recv_sem=recv_sem.at[parity, number],
-                device_id=device(dev_y, dev_z), device_id_type=MESH))
-
-        inner = pl.ds(first_row, nz)
-        without_first, without_last = pl.ds(first_row + 1, nz - 1), pl.ds(first_row, nz - 1)
-        for slots, rows in ((pl.ds(1, 3), inner), (pl.ds(4, 1), without_first), (pl.ds(0, 1), without_last)):
-            add(state.at[slots, ny, :, rows, :], state.at[slots, 0, :, rows, :], up_y, me_z)
-        for slots, rows in ((pl.ds(9, 3), inner), (pl.ds(8, 1), without_first), (pl.ds(12, 1), without_last)):
-            add(state.at[slots, 1, :, rows, :], state.at[slots, ny + 1, :, rows, :], down_y, me_z)
-        all_planes, lower_planes, upper_planes = pl.ds(1, ny), pl.ds(1, ny - 1), pl.ds(2, ny - 1)
-        out_up, out_down = pl.ds(last_row + 1, 1), pl.ds(first_row - 1, 1)
-        in_up, in_down = pl.ds(first_row, 1), pl.ds(last_row, 1)
-        for slots, planes in ((pl.ds(5, 3), all_planes), (pl.ds(4, 1), lower_planes), (pl.ds(8, 1), upper_planes)):
-            add(state.at[slots, planes, :, out_up, :], state.at[slots, planes, :, in_up, :], me_y, up_z)
-        for slots, planes in ((pl.ds(13, 3), all_planes), (pl.ds(0, 1), lower_planes), (pl.ds(12, 1), upper_planes)):
-            add(state.at[slots, planes, :, out_down, :], state.at[slots, planes, :, in_down, :], me_y, down_z)
-        add(state.at[4, ny, :, out_up, :], state.at[4, 0, :, in_up, :], up_y, up_z)
-        add(state.at[0, ny, :, out_down, :], state.at[0, 0, :, in_down, :], up_y, down_z)
-        add(state.at[8, 1, :, out_up, :], state.at[8, ny + 1, :, in_up, :], down_y, up_z)
-        add(state.at[12, 1, :, out_down, :], state.at[12, ny + 1, :, in_down, :], down_y, down_z)
+                src_ref=state.at[slots, source, :, rows, :], dst_ref=state.at[slots, target, :, rows, :],
+                send_sem=face_send.at[parity, face, tile], recv_sem=face_recv.at[parity, face, tile],
+                device_id=device(dev_y, me_z), device_id_type=MESH))
         return result
 
-    def over(count, body):
+    def edges(step):
+        state, parity = buffers[step % 2], step % 2
+        planes = pl.ds(1, ny)
+        low, high, below, above = (pl.ds(row, 1) for row in (ROWS, ROWS + nz - 1, ROWS - 1, ROWS + nz))
+        parts = (
+            (0, ny, low, 0, above, up_y, down_z),
+            (12, 1, low, ny + 1, above, down_y, down_z),
+            (pl.ds(12, 4), planes, low, planes, above, me_y, down_z),
+            (0, planes, low, planes, above, me_y, down_z),
+            (4, ny, high, 0, below, up_y, up_z),
+            (8, 1, high, ny + 1, below, down_y, up_z),
+            (pl.ds(4, 5), planes, high, planes, below, me_y, up_z),
+        )
+        return [pltpu.make_async_remote_copy(
+            src_ref=state.at[slots, source, :, source_row, :], dst_ref=state.at[slots, target, :, target_row, :],
+            send_sem=edge_send.at[parity, number], recv_sem=edge_recv.at[parity, number],
+            device_id=device(dev_y, dev_z), device_id_type=MESH)
+            for number, (slots, source, source_row, target, target_row, dev_y, dev_z) in enumerate(parts)]
+
+    def over(start, stop, body):
         def run(index, carry):
             body(index)
             return carry
-        lax.fori_loop(0, count, run, 0)
-
-    started = [copies(step) for step in range(STEPS)]
+        lax.fori_loop(start, stop, run, 0)
+
+    all_edges = [edges(step) for step in range(STEPS)]
     for step in range(STEPS):
+        now = all_edges[step]
         if step == 0:
             loads[0].wait()
             loads[ny - 1].wait()
-        else:
-            for copy in started[step - 1]:
+
+        def await_piece(tile):
+            for copy in faces(step - 1, tile):
                 copy.wait_recv()
-        if step >= 2:
-            for copy in started[step - 2]:
+
+        def place(position):
+            upward = position % 2 == 0
+            tile = jnp.where(upward, position // 2, tiles - 1 - position // 2)
+            if step > 0:
+                @pl.when(position < 2)
+                def _():
+                    await_piece(tile)
+                @pl.when(position < tiles - 2)
+                def _():
+                    await_piece(jnp.where(upward, tile + 1, tile - 1))
+                @pl.when(position == 0)
+                def _():
+                    for copy in all_edges[step - 1][:4]:
+                        copy.wait_recv()
+                    for copy in all_edges[step - 1][4:]:
+                        copy.wait_recv()
+            if step >= 2:
+                for copy in faces(step - 2, tile):
+                    copy.wait_send()
+                @pl.when(position == 0)
+                def _():
+                    for copy in all_edges[step - 2]:
+                        copy.wait_send()
+            over(0, 2, lambda index: collide_tile(step, index * (ny - 1), tile))
+            if step == 0:
+                @pl.when(position == 0)
+                def _():
+                    pl.semaphore_wait(barrier, len(neighbours))
+            for number in range(2):
+                @pl.when(position == number)
+                def _():
+                    for copy in (now[0:2], now[4:6])[number]:
+                        copy.start()
+            for copy in faces(step, tile):
+                copy.start()
+            if step == 0:
+                @pl.when(position == 0)
+                def _():
+                    for y in range(1, ny - 1):
+                        loads[y].wait()
+            over(1, ny - 1, lambda index: collide_tile(step, index, tile))
+            for number in range(2):
+                @pl.when(position == number)
+                def _():
+                    for copy in (now[2:4], now[6:7])[number]:
+                        copy.start()
+
+        over(0, tiles, place)
+
+    def await_last(tile):
+        for copy in faces(STEPS - 1, tile):
+            copy.wait_recv()
+        for step in (STEPS - 2, STEPS - 1):
+            for copy in faces(step, tile):
                 copy.wait_send()
-        over(2 * tiles, lambda index: collide_tile(step, (index // tiles) * (ny - 1), index % tiles))
-        if step == 0:
-            pl.semaphore_wait(barrier, len(neighbours))
-        for copy in started[step][:6]:
-            copy.start()
-        if step == 0:
-            for y in range(1, ny - 1):
-                loads[y].wait()
-        over(2 * (ny - 2), lambda index: collide_tile(step, 1 + index // 2, (index % 2) * (tiles - 1)))
-        for copy in started[step][6:]:
-            copy.start()
-        over((ny - 2) * (tiles - 2), lambda index: collide_tile(step, 1 + index // (tiles - 2), 1 + index % (tiles - 2)))
-    for copy in started[STEPS - 1]:
+
+    over(0, tiles, await_last)
+    for copy in all_edges[STEPS - 1]:
         copy.wait_recv()
     for step in (STEPS - 2, STEPS - 1):
-        for copy in started[step]:
+        for copy in all_edges[step]:
             copy.wait_send()
 
 
 def output_kernel(ny, nz, tau_ref, force_ref, state, field_ref, density_ref, velocity_ref, moments, field_sem, moment_sem):
     field_copies = []
     for pop_id in range(19):
-        shift_y = VELOCITIES[pop_id][1]
+        _, shift_y, shift_z = VELOCITIES[pop_id]
         for half in range(2):
             field_copies.append(pltpu.make_async_copy(
-                state.at[SLOT[pop_id], pl.ds(1 - shift_y, ny), half, pl.ds(ROWS, nz), :],
+                state.at[SLOT[pop_id], pl.ds(1 - shift_y, ny), half, pl.ds(ROWS - shift_z, nz), :],
                 field_ref.at[pop_id, :, :, pl.ds(half * LANES, LANES)], field_sem.at[2 * pop_id + half]))
     for copy in field_copies:
         copy.start()
@@ -208,7 +252,8 @@
             row = pl.multiple_of(tile * ROWS, ROWS)
             for half in range(2):
                 def load(pop_id):
-                    return state[SLOT[pop_id], y + 1 - VELOCITIES[pop_id][1], half, pl.ds(row + ROWS, ROWS), :]
+                    _, shift_y, shift_z = VELOCITIES[pop_id]
+                    return state[SLOT[pop_id], y + 1 - shift_y, half, pl.ds(row + (ROWS - shift_z), ROWS), :]
                 density, momentum = moment_sums(load)
                 inverse = 1.0 / density
                 place = (y, pl.ds(row, ROWS), pl.ds(half * LANES, LANES))
@@ -248,8 +293,10 @@
                 pltpu.VMEM((19, ny, nz, nx), jnp.float32),
                 pltpu.VMEM(state_shape, jnp.float32),
                 pltpu.SemaphoreType.DMA((ny,)),
-                pltpu.SemaphoreType.DMA((2, COPIES)),
-                pltpu.SemaphoreType.DMA((2, COPIES)),
+                pltpu.SemaphoreType.DMA((2, 2, nz // ROWS)),
+                pltpu.SemaphoreType.DMA((2, 2, nz // ROWS)),
+                pltpu.SemaphoreType.DMA((2, EDGE_COPIES)),
+                pltpu.SemaphoreType.DMA((2, EDGE_COPIES)),
             ],
             compiler_params=pltpu.CompilerParams(collective_id=0, has_side_effects=True, vmem_limit_bytes=44 * 2**20),
         )(tau, body_force, field)

time: 54.5 us -> 50.1 us (0.919)
  Pallas kernels: 53 us -> 48.6 us
    pallas_call x1, Pallas kernels: 47.6 us -> 43.3 us  [local_steps(): pl.pallas_call(functools.partial(step_kernel, size_y, size_z, ny, nz), na...]
where the time goes in v1:
time: 50.1 us; the launch traced here: 49.9 us
  Pallas kernels  48.6 us (97%)
  between operations  1.3 us (3%)
    pallas_call x1, Pallas kernels, local_steps(): pl.pallas_call(functools.partial(step_kernel, size_y, size_z, ny, nz), na...  43.3 us
    pallas_call x1, Pallas kernels, local_steps(): pl.pallas_call(functools.partial(output_kernel, ny, nz), name='lattice_ou...  5.37 us

profile of v1, /device:TPU:0, one launch (start us, length us, event | category | flops | bytes accessed | tf_op | source)
XLA Modules:
  0.0 49.9 jit_solution(15469544029326691631)
XLA Ops:
  1.3 0.0 copy-start
  1.3 43.3 %lattice_steps.1.state = f32[19,10,2,80,128]{4,3,2,1,0:T(8,128)S(1)} custom-call(f32[1]{0:T(128)} %bitcast.5.tau_ref, f32[3]{0:T(128)} %force_ref.3, f32[19,8,64,256]{3,2,1,0:T(8,128)} %bitcast.7), custom_call_target="tpu_custom_call" | custom-call | tf_op jit(solution)/shard_map/lattice_steps/pallas_call | solution.py:286
  44.5 0.0 copy-done
  44.6 5.4 %lattice_output.1 = (f32[19,8,64,256]{3,2,1,0:T(8,128)}, f32[8,64,256]{2,1,0:T(8,128)}, f32[3,8,64,256]{3,2,1,0:T(8,128)}) custom-call(f32[1]{0:T(128)} %bitcast.6.tau_ref, f32[3]{0:T(128)S(1)} %copy-done, f32[19,10,2,80,128]{4,3,2,1,0:T(8,128)S(1)} %lattice_steps.1.state), custom_call_target="tpu_custom_call" | custom-call | tf_op jit(solution)/shard_map/lattice_output/pallas_call | solution.py:303
Async XLA Ops:
  1.3 43.3 %copy-start = (f32[3]{0:T(128)S(1)}, f32[3]{0:T(128)}, u32[]{:S(2)}) copy-start(f32[3]{0:T(128)} %force_ref.3) | copy-start | bytes 40

commit v2 on v1

--- a/solution.py
+++ b/solution.py
@@ -70,7 +70,7 @@
     return [jnp.where(edge, moved[1], moved[0]), jnp.where(edge, moved[0], moved[1])]
 
 
-def step_kernel(size_y, size_z, ny, nz, tau_ref, force_ref, field_ref, out_ref, stage, other, load_sem, face_send, face_recv, edge_send, edge_recv):
+def step_kernel(size_y, size_z, ny, nz, tau_in, force_in, field_ref, out_ref, stage, other, tau_ref, force_ref, param_sem, load_sem, first_sem, face_send, face_recv, edge_send, edge_recv):
     me_y, me_z = lax.axis_index("py"), lax.axis_index("pz")
     up_y, down_y = lax.rem(me_y + 1, size_y), lax.rem(me_y + size_y - 1, size_y)
     up_z, down_z = lax.rem(me_z + 1, size_z), lax.rem(me_z + size_z - 1, size_z)
@@ -84,10 +84,23 @@
     for neighbour in neighbours:
         pl.semaphore_signal(barrier, inc=1, device_id=neighbour, device_id_type=MESH)
 
-    plane_order = [0, ny - 1] + list(range(1, ny - 1))
-    loads = {y: pltpu.make_async_copy(field_ref.at[:, y], stage.at[:, y], load_sem.at[y]) for y in plane_order}
-    for y in plane_order:
-        loads[y].start()
+    tiles = nz // ROWS
+    params = [pltpu.make_async_copy(tau_in, tau_ref, param_sem.at[0]), pltpu.make_async_copy(force_in, force_ref, param_sem.at[1])]
+    for copy in params:
+        copy.start()
+
+    def first_loads(tile):
+        rows = pl.ds(pl.multiple_of(tile * ROWS, ROWS), ROWS)
+        return [pltpu.make_async_copy(field_ref.at[:, y, rows], stage.at[:, y, rows], first_sem.at[face, tile]) for face, y in enumerate((0, ny - 1))]
+
+    for position in range(tiles):
+        for copy in first_loads(position // 2 if position % 2 == 0 else tiles - 1 - position // 2):
+            copy.start()
+    loads = [pltpu.make_async_copy(field_ref.at[:, y], stage.at[:, y], load_sem.at[y]) for y in range(1, ny - 1)]
+    for copy in loads:
+        copy.start()
+    for copy in params:
+        copy.wait()
 
     tau = jnp.full((ROWS, LANES), tau_ref[0], jnp.float32)
     rate = 1.0 / tau
@@ -96,7 +109,6 @@
     force = [tau * force_ref[axis] for axis in range(3)]
     lane = lax.broadcasted_iota(jnp.int32, (ROWS, LANES), 1)
     buffers = (other, out_ref)
-    tiles = nz // ROWS
 
     def collide_tile(step, y, tile):
         row = pl.multiple_of(tile * ROWS, ROWS)
@@ -152,19 +164,15 @@
             device_id=device(dev_y, dev_z), device_id_type=MESH)
             for number, (slots, source, source_row, target, target_row, dev_y, dev_z) in enumerate(parts)]
 
-    def over(start, stop, body):
+    def over(start, stop, body, unroll=False):
         def run(index, carry):
             body(index)
             return carry
-        lax.fori_loop(start, stop, run, 0)
+        lax.fori_loop(start, stop, run, 0, unroll=unroll)
 
     all_edges = [edges(step) for step in range(STEPS)]
     for step in range(STEPS):
         now = all_edges[step]
-        if step == 0:
-            loads[0].wait()
-            loads[ny - 1].wait()
-
         def await_piece(tile):
             for copy in faces(step - 1, tile):
                 copy.wait_recv()
@@ -172,6 +180,9 @@
         def place(position):
             upward = position % 2 == 0
             tile = jnp.where(upward, position // 2, tiles - 1 - position // 2)
+            if step == 0:
+                for copy in first_loads(tile):
+                    copy.wait()
             if step > 0:
                 @pl.when(position < 2)
                 def _():
@@ -192,7 +203,7 @@
                 def _():
                     for copy in all_edges[step - 2]:
                         copy.wait_send()
-            over(0, 2, lambda index: collide_tile(step, index * (ny - 1), tile))
+            over(0, 2, lambda index: collide_tile(step, index * (ny - 1), tile), True)
             if step == 0:
                 @pl.when(position == 0)
                 def _():
@@ -207,9 +218,9 @@
             if step == 0:
                 @pl.when(position == 0)
                 def _():
-                    for y in range(1, ny - 1):
-                        loads[y].wait()
-            over(1, ny - 1, lambda index: collide_tile(step, index, tile))
+                    for copy in loads:
+                        copy.wait()
+            over(1, ny - 1, lambda index: collide_tile(step, index, tile), True)
             for number in range(2):
                 @pl.when(position == number)
                 def _():
@@ -233,7 +244,10 @@
             copy.wait_send()
 
 
-def output_kernel(ny, nz, tau_ref, force_ref, state, field_ref, density_ref, velocity_ref, moments, field_sem, moment_sem):
+def output_kernel(ny, nz, tau_in, force_in, state, field_ref, density_ref, velocity_ref, moments, tau_ref, force_ref, param_sem, field_sem, moment_sem):
+    params = [pltpu.make_async_copy(tau_in, tau_ref, param_sem.at[0]), pltpu.make_async_copy(force_in, force_ref, param_sem.at[1])]
+    for copy in params:
+        copy.start()
     field_copies = []
     for pop_id in range(19):
         _, shift_y, shift_z = VELOCITIES[pop_id]
@@ -243,6 +257,8 @@
                 field_ref.at[pop_id, :, :, pl.ds(half * LANES, LANES)], field_sem.at[2 * pop_id + half]))
     for copy in field_copies:
         copy.start()
+    for copy in params:
+        copy.wait()
     tau = jnp.full((ROWS, LANES), tau_ref[0], jnp.float32)
     force = [tau * force_ref[axis] for axis in range(3)]
     tiles = nz // ROWS
@@ -280,19 +296,22 @@
         _, ny, nz, nx = field.shape
         tau = jnp.reshape(relax_time, (1,))
         state_shape = (19, ny + 2, 2, nz + 2 * ROWS, LANES)
-        smem = pl.BlockSpec(memory_space=pltpu.SMEM)
         vmem = pl.BlockSpec(memory_space=pltpu.VMEM)
         anywhere = pl.BlockSpec(memory_space=pl.ANY)
         state = pl.pallas_call(
             functools.partial(step_kernel, size_y, size_z, ny, nz),
             name="lattice_steps",
             out_shape=pltpu.VMEM(state_shape, jnp.float32),
-            in_specs=[smem, smem, anywhere],
+            in_specs=[anywhere, anywhere, anywhere],
             out_specs=vmem,
             scratch_shapes=[
                 pltpu.VMEM((19, ny, nz, nx), jnp.float32),
                 pltpu.VMEM(state_shape, jnp.float32),
+                pltpu.SMEM((1,), jnp.float32),
+                pltpu.SMEM((3,), jnp.float32),
+                pltpu.SemaphoreType.DMA((2,)),
                 pltpu.SemaphoreType.DMA((ny,)),
+                pltpu.SemaphoreType.DMA((2, nz // ROWS)),
                 pltpu.SemaphoreType.DMA((2, 2, nz // ROWS)),
                 pltpu.SemaphoreType.DMA((2, 2, nz // ROWS)),
                 pltpu.SemaphoreType.DMA((2, EDGE_COPIES)),
@@ -308,10 +327,13 @@
                 jax.ShapeDtypeStruct((ny, nz, nx), jnp.float32),
                 jax.ShapeDtypeStruct((3, ny, nz, nx), jnp.float32),
             ),
-            in_specs=[smem, smem, vmem],
+            in_specs=[anywhere, anywhere, vmem],
             out_specs=(anywhere, anywhere, anywhere),
             scratch_shapes=[
                 pltpu.VMEM((4, ny, nz, nx), jnp.float32),
+                pltpu.SMEM((1,), jnp.float32),
+                pltpu.SMEM((3,), jnp.float32),
+                pltpu.SemaphoreType.DMA((2,)),
                 pltpu.SemaphoreType.DMA((38,)),
                 pltpu.SemaphoreType.DMA((2, ny)),
             ],

time: 50.1 us -> 43.8 us (0.87)
  Pallas kernels: 48.6 us -> 42.4 us
    pallas_call x1, Pallas kernels: 43.3 us -> 37.5 us  [local_steps(): pl.pallas_call(functools.partial(step_kernel, size_y, size_z, ny, nz), na...]
    pallas_call x1, Pallas kernels: 5.37 us -> 4.85 us  [local_steps(): pl.pallas_call(functools.partial(output_kernel, ny, nz), name='lattice_ou...]
where the time goes in v2:
time: 43.8 us; the launch traced here: 43.7 us
  Pallas kernels  42.4 us (97%)
  between operations  1.3 us (3%)
    pallas_call x1, Pallas kernels, local_steps(): pl.pallas_call(functools.partial(step_kernel, size_y, size_z, ny, nz), na...  37.5 us
    pallas_call x1, Pallas kernels, local_steps(): pl.pallas_call(functools.partial(output_kernel, ny, nz), name='lattice_ou...  4.85 us

profile of v2, /device:TPU:0, one launch (start us, length us, event | category | flops | bytes accessed | tf_op | source)
XLA Modules:
  0.0 43.7 jit_solution(15743169596143930072)
XLA Ops:
  1.3 0.0 copy-start
  1.3 37.5 %lattice_steps.1.state = f32[19,10,2,80,128]{4,3,2,1,0:T(8,128)S(1)} custom-call(f32[1]{0:T(128)} %bitcast.5.tau_in, f32[3]{0:T(128)} %force_in.3, f32[19,8,64,256]{3,2,1,0:T(8,128)} %bitcast.7), custom_call_target="tpu_custom_call" | custom-call | tf_op jit(solution)/shard_map/lattice_steps/pallas_call | solution.py:301
  38.8 0.0 copy-done
  38.8 4.9 %lattice_output.1 = (f32[19,8,64,256]{3,2,1,0:T(8,128)}, f32[8,64,256]{2,1,0:T(8,128)}, f32[3,8,64,256]{3,2,1,0:T(8,128)}) custom-call(f32[1]{0:T(128)} %bitcast.6.tau_in, f32[3]{0:T(128)S(1)} %copy-done, f32[19,10,2,80,128]{4,3,2,1,0:T(8,128)S(1)} %lattice_steps.1.state), custom_call_target="tpu_custom_call" | custom-call | tf_op jit(solution)/shard_map/lattice_output/pallas_call | solution.py:322
Async XLA Ops:
  1.3 37.5 %copy-start = (f32[3]{0:T(128)S(1)}, f32[3]{0:T(128)}, u32[]{:S(2)}) copy-start(f32[3]{0:T(128)} %force_in.3) | copy-start | bytes 40

commit v3 on v2

--- a/solution.py
+++ b/solution.py
@@ -70,7 +70,7 @@
     return [jnp.where(edge, moved[1], moved[0]), jnp.where(edge, moved[0], moved[1])]
 
 
-def step_kernel(size_y, size_z, ny, nz, tau_in, force_in, field_ref, out_ref, stage, other, tau_ref, force_ref, param_sem, load_sem, first_sem, face_send, face_recv, edge_send, edge_recv):
+def step_kernel(size_y, size_z, ny, nz, tau_in, force_in, field_ref, stage, density_ref, velocity_ref, buffer_0, buffer_1, tau_ref, force_ref, param_sem, load_sem, first_sem, face_send, face_recv, edge_send, edge_recv):
     me_y, me_z = lax.axis_index("py"), lax.axis_index("pz")
     up_y, down_y = lax.rem(me_y + 1, size_y), lax.rem(me_y + size_y - 1, size_y)
     up_z, down_z = lax.rem(me_z + 1, size_z), lax.rem(me_z + size_z - 1, size_z)
@@ -108,7 +108,7 @@
     rate36 = rate * (1.0 / 36.0)
     force = [tau * force_ref[axis] for axis in range(3)]
     lane = lax.broadcasted_iota(jnp.int32, (ROWS, LANES), 1)
-    buffers = (other, out_ref)
+    buffers = (buffer_0, buffer_1)
 
     def collide_tile(step, y, tile):
         row = pl.multiple_of(tile * ROWS, ROWS)
@@ -170,32 +170,89 @@
             return carry
         lax.fori_loop(start, stop, run, 0, unroll=unroll)
 
+    def finish_tile(y, tile):
+        row = pl.multiple_of(tile * ROWS, ROWS)
+        source = buffers[(STEPS - 1) % 2]
+        for half in range(2):
+            place = (y, pl.ds(row, ROWS), pl.ds(half * LANES, LANES))
+
+            def load(pop_id):
+                _, shift_y, shift_z = VELOCITIES[pop_id]
+                value = source[SLOT[pop_id], y + 1 - shift_y, half, pl.ds(row + (ROWS - shift_z), ROWS), :]
+                stage[(pop_id, *place)] = value
+                return value
+
+            density, momentum = moment_sums(load)
+            density_ref[place] = density
+            for axis in range(3):
+                velocity_ref[(axis, *place)] = (momentum[axis] + force[axis]) / density
+
+    def tile_at(position):
+        return jnp.where(position % 2 == 0, position // 2, tiles - 1 - position // 2)
+
+    def at_position(position, number, copies):
+        @pl.when(position == number)
+        def _():
+            for copy in copies:
+                copy.start()
+
     all_edges = [edges(step) for step in range(STEPS)]
-    for step in range(STEPS):
-        now = all_edges[step]
-        def await_piece(tile):
-            for copy in faces(step - 1, tile):
+
+    def collide_faces(step, tile):
+        over(0, 2, lambda index: collide_tile(step, index * (ny - 1), tile), True)
+
+    def collide_inner(step, tile):
+        over(1, ny - 1, lambda index: collide_tile(step, index, tile), True)
+
+    def start_faces(step, position, tile):
+        at_position(position, 0, all_edges[step][0:2])
+        at_position(position, 1, all_edges[step][4:6])
+        for copy in faces(step, tile):
+            copy.start()
+
+    def start_rows(step, position):
+        at_position(position, 0, all_edges[step][2:4])
+        at_position(position, 1, all_edges[step][6:7])
+
+    def await_pieces(step, position, tile):
+        def await_piece(number):
+            for copy in faces(step, number):
                 copy.wait_recv()
 
+        @pl.when(position < 2)
+        def _():
+            await_piece(tile)
+        @pl.when(position < tiles - 2)
+        def _():
+            await_piece(jnp.where(position % 2 == 0, tile + 1, tile - 1))
+
+    def first_faces(position):
+        tile = tile_at(position)
+        for copy in first_loads(tile):
+            copy.wait()
+        collide_faces(0, tile)
+        @pl.when(position == 0)
+        def _():
+            pl.semaphore_wait(barrier, len(neighbours))
+        start_faces(0, position, tile)
+
+    def first_inner(position):
+        collide_inner(0, tile_at(position))
+        start_rows(0, position)
+
+    over(0, tiles, first_faces)
+    for copy in loads:
+        copy.wait()
+    over(0, tiles, first_inner)
+
+    for step in range(1, STEPS):
         def place(position):
-            upward = position % 2 == 0
-            tile = jnp.where(upward, position // 2, tiles - 1 - position // 2)
-            if step == 0:
-                for copy in first_loads(tile):
-                    copy.wait()
-            if step > 0:
-                @pl.when(position < 2)
-                def _():
-                    await_piece(tile)
-                @pl.when(position < tiles - 2)
-                def _():
-                    await_piece(jnp.where(upward, tile + 1, tile - 1))
-                @pl.when(position == 0)
-                def _():
-                    for copy in all_edges[step - 1][:4]:
-                        copy.wait_recv()
-                    for copy in all_edges[step - 1][4:]:
-                        copy.wait_recv()
+            tile = tile_at(position)
+            await_pieces(step - 1, position, tile)
+            @pl.when(position == 0)
+            def _():
+                for copy in all_edges[step - 1]:
+                    copy.wait_recv()
             if step >= 2:
                 for copy in faces(step - 2, tile):
                     copy.wait_send()
@@ -203,86 +260,43 @@
                 def _():
                     for copy in all_edges[step - 2]:
                         copy.wait_send()
-            over(0, 2, lambda index: collide_tile(step, index * (ny - 1), tile), True)
-            if step == 0:
-                @pl.when(position == 0)
-                def _():
-                    pl.semaphore_wait(barrier, len(neighbours))
-            for number in range(2):
-                @pl.when(position == number)
-                def _():
-                    for copy in (now[0:2], now[4:6])[number]:
-                        copy.start()
-            for copy in faces(step, tile):
-                copy.start()
-            if step == 0:
-                @pl.when(position == 0)
-                def _():
-                    for copy in loads:
-                        copy.wait()
-            over(1, ny - 1, lambda index: collide_tile(step, index, tile), True)
-            for number in range(2):
-                @pl.when(position == number)
-                def _():
-                    for copy in (now[2:4], now[6:7])[number]:
-                        copy.start()
+            collide_faces(step, tile)
+            start_faces(step, position, tile)
+            collide_inner(step, tile)
+            start_rows(step, position)
 
         over(0, tiles, place)
 
-    def await_last(tile):
-        for copy in faces(STEPS - 1, tile):
-            copy.wait_recv()
-        for step in (STEPS - 2, STEPS - 1):
+    last = STEPS - 1
+    for copy in all_edges[last]:
+        copy.wait_recv()
+    over(0, tiles, lambda tile: over(1, ny - 1, lambda y: finish_tile(y, tile)))
+
+    def finish_faces(position):
+        tile = tile_at(position)
+        await_pieces(last, position, tile)
+        over(0, 2, lambda index: finish_tile(index * (ny - 1), tile))
+
+    over(0, tiles, finish_faces)
+
+    def await_sends(tile):
+        for step in (last - 1, last):
             for copy in faces(step, tile):
                 copy.wait_send()
 
-    over(0, tiles, await_last)
-    for copy in all_edges[STEPS - 1]:
-        copy.wait_recv()
-    for step in (STEPS - 2, STEPS - 1):
+    over(0, tiles, await_sends)
+    for step in (last - 1, last):
         for copy in all_edges[step]:
             copy.wait_send()
 
 
-def output_kernel(ny, nz, tau_in, force_in, state, field_ref, density_ref, velocity_ref, moments, tau_ref, force_ref, param_sem, field_sem, moment_sem):
-    params = [pltpu.make_async_copy(tau_in, tau_ref, param_sem.at[0]), pltpu.make_async_copy(force_in, force_ref, param_sem.at[1])]
-    for copy in params:
+def output_kernel(final_in, density_in, velocity_in, final_ref, density_ref, velocity_ref, final_sem, moment_sem):
+    copies = [pltpu.make_async_copy(final_in.at[pop_id], final_ref.at[pop_id], final_sem.at[pop_id]) for pop_id in range(19)]
+    copies.append(pltpu.make_async_copy(density_in, density_ref, moment_sem.at[0]))
+    copies.append(pltpu.make_async_copy(velocity_in, velocity_ref, moment_sem.at[1]))
+    for copy in copies:
         copy.start()
-    field_copies = []
-    for pop_id in range(19):
-        _, shift_y, shift_z = VELOCITIES[pop_id]
-        for half in range(2):
-            field_copies.append(pltpu.make_async_copy(
-                state.at[SLOT[pop_id], pl.ds(1 - shift_y, ny), half, pl.ds(ROWS - shift_z, nz), :],
-                field_ref.at[pop_id, :, :, pl.ds(half * LANES, LANES)], field_sem.at[2 * pop_id + half]))
-    for copy in field_copies:
-        copy.start()
-    for copy in params:
-        copy.wait()
-    tau = jnp.full((ROWS, LANES), tau_ref[0], jnp.float32)
-    force = [tau * force_ref[axis] for axis in range(3)]
-    tiles = nz // ROWS
-    moment_copies = []
-    for y in range(ny):
-        def tile_moments(tile, carry):
-            row = pl.multiple_of(tile * ROWS, ROWS)
-            for half in range(2):
-                def load(pop_id):
-                    _, shift_y, shift_z = VELOCITIES[pop_id]
-                    return state[SLOT[pop_id], y + 1 - shift_y, half, pl.ds(row + (ROWS - shift_z), ROWS), :]
-                density, momentum = moment_sums(load)
-                inverse = 1.0 / density
-                place = (y, pl.ds(row, ROWS), pl.ds(half * LANES, LANES))
-                moments[(0, *place)] = density
-                for axis in range(3):
-                    moments[(1 + axis, *place)] = (momentum[axis] + force[axis]) * inverse
-            return carry
-        lax.fori_loop(0, tiles, tile_moments, 0)
-        moment_copies.append(pltpu.make_async_copy(moments.at[0, y], density_ref.at[y], moment_sem.at[0, y]))
-        moment_copies.append(pltpu.make_async_copy(moments.at[pl.ds(1, 3), y], velocity_ref.at[:, y], moment_sem.at[1, y]))
-        moment_copies[-2].start()
-        moment_copies[-1].start()
-    for copy in field_copies + moment_copies:
+    for copy in copies:
         copy.wait()
 
 
@@ -298,14 +312,18 @@
         state_shape = (19, ny + 2, 2, nz + 2 * ROWS, LANES)
         vmem = pl.BlockSpec(memory_space=pltpu.VMEM)
         anywhere = pl.BlockSpec(memory_space=pl.ANY)
-        state = pl.pallas_call(
+        results = pl.pallas_call(
             functools.partial(step_kernel, size_y, size_z, ny, nz),
             name="lattice_steps",
-            out_shape=pltpu.VMEM(state_shape, jnp.float32),
+            out_shape=(
+                pltpu.VMEM((19, ny, nz, nx), jnp.float32),
+                pltpu.VMEM((ny, nz, nx), jnp.float32),
+                pltpu.VMEM((3, ny, nz, nx), jnp.float32),
+            ),
             in_specs=[anywhere, anywhere, anywhere],
-            out_specs=vmem,
+            out_specs=(vmem, vmem, vmem),
             scratch_shapes=[
-                pltpu.VMEM((19, ny, nz, nx), jnp.float32),
+                pltpu.VMEM(state_shape, jnp.float32),
                 pltpu.VMEM(state_shape, jnp.float32),
                 pltpu.SMEM((1,), jnp.float32),
                 pltpu.SMEM((3,), jnp.float32),
@@ -317,28 +335,17 @@
                 pltpu.SemaphoreType.DMA((2, EDGE_COPIES)),
                 pltpu.SemaphoreType.DMA((2, EDGE_COPIES)),
             ],
-            compiler_params=pltpu.CompilerParams(collective_id=0, has_side_effects=True, vmem_limit_bytes=44 * 2**20),
+            compiler_params=pltpu.CompilerParams(collective_id=0, has_side_effects=True, vmem_limit_bytes=46 * 2**20),
         )(tau, body_force, field)
         final, density, velocity = pl.pallas_call(
-            functools.partial(output_kernel, ny, nz),
+            output_kernel,
             name="lattice_output",
-            out_shape=(
-                jax.ShapeDtypeStruct((19, ny, nz, nx), jnp.float32),
-                jax.ShapeDtypeStruct((ny, nz, nx), jnp.float32),
-                jax.ShapeDtypeStruct((3, ny, nz, nx), jnp.float32),
-            ),
-            in_specs=[anywhere, anywhere, vmem],
+            out_shape=tuple(jax.ShapeDtypeStruct(result.shape, result.dtype) for result in results),
+            in_specs=[vmem, vmem, vmem],
             out_specs=(anywhere, anywhere, anywhere),
-            scratch_shapes=[
-                pltpu.VMEM((4, ny, nz, nx), jnp.float32),
-                pltpu.SMEM((1,), jnp.float32),
-                pltpu.SMEM((3,), jnp.float32),
-                pltpu.SemaphoreType.DMA((2,)),
-                pltpu.SemaphoreType.DMA((38,)),
-                pltpu.SemaphoreType.DMA((2, ny)),
-            ],
-            compiler_params=pltpu.CompilerParams(vmem_limit_bytes=24 * 2**20),
-        )(tau, body_force, state)
+            scratch_shapes=[pltpu.SemaphoreType.DMA((19,)), pltpu.SemaphoreType.DMA((2,))],
+            compiler_params=pltpu.CompilerParams(vmem_limit_bytes=2**20),
+        )(*results)
         return jnp.transpose(final, (0, 3, 1, 2)), jnp.transpose(density, (2, 0, 1)), jnp.transpose(velocity, (0, 3, 1, 2))
 
     return jax.shard_map(local_steps, mesh=mesh, in_specs=(field_spec, P(), P()), out_specs=(field_spec, P(None, "py", "pz"), field_spec), check_vma=False)

time: 43.8 us -> 43.8 us (level)
  no operation moved by 1% of the time
where the time goes in v3:
time: 43.8 us; the launch traced here: 43.6 us
  Pallas kernels  42.3 us (97%)
  between operations  1.28 us (3%)
    pallas_call x1, Pallas kernels, local_steps(): pl.pallas_call(functools.partial(step_kernel, size_y, size_z, ny, nz), na...  37.7 us
    pallas_call x1, Pallas kernels, local_steps(): pl.pallas_call(output_kernel, name='lattice_output', out_shape=tuple((jax...  4.6 us

profile of v3, /device:TPU:0, one launch (start us, length us, event | category | flops | bytes accessed | tf_op | source)
XLA Modules:
  0.0 43.6 jit_solution(1724619487090508728)
XLA Ops:
  1.3 37.7 %lattice_steps.1 = (f32[19,8,64,256]{3,2,1,0:T(8,128)S(1)}, f32[8,64,256]{2,1,0:T(8,128)S(1)}, f32[3,8,64,256]{3,2,1,0:T(8,128)S(1)}) custom-call(f32[1]{0:T(128)} %bitcast.5.tau_in, f32[3]{0:T(128)} %force_in.1, f32[19,8,64,256]{3,2,1,0:T(8,128)} %bitcast.6), custom_call_target="tpu_custom_call" | custom-call | tf_op jit(solution)/shard_map/lattice_steps/pallas_call | solution.py:315
  39.0 4.6 %lattice_output.1 = (f32[19,8,64,256]{3,2,1,0:T(8,128)}, f32[8,64,256]{2,1,0:T(8,128)}, f32[3,8,64,256]{3,2,1,0:T(8,128)}) custom-call(f32[19,8,64,256]{3,2,1,0:T(8,128)S(1)} %get-tuple-element.9.final_in, f32[8,64,256]{2,1,0:T(8,128)S(1)} %get-tuple-element.10.density_in, f32[3,8,64,256]{3,2,1,0:T(8,128)S(1)} %get-tuple-element.11.velocity_in), custom_call_target="tpu_custom_call" | custom-call | tf_op jit(solution)/shard_map/lattice_output/pallas_call | solution.py:340

commit v4 on v3

--- a/solution.py
+++ b/solution.py
@@ -79,10 +79,29 @@
         return {"py": dev_y, "pz": dev_z}
 
     barrier = pltpu.get_barrier_semaphore()
-    neighbours = [device(dy, dz) for dy in (down_y, me_y, up_y) for dz in (down_z, me_z, up_z)]
-    del neighbours[4]
-    for neighbour in neighbours:
-        pl.semaphore_signal(barrier, inc=1, device_id=neighbour, device_id_type=MESH)
+    beside = [(dev_y, dev_z) for dev_z in (down_z, up_z) for dev_y in (down_y, me_y, up_y)]
+
+    def signal(dev_y, dev_z):
+        pl.semaphore_signal(barrier, inc=1, device_id=device(dev_y, dev_z), device_id_type=MESH)
+
+    signal(up_y, me_z)
+    signal(down_y, me_z)
+    for dev_y, dev_z in beside:
+        @pl.when(jnp.logical_and(me_z != 0, dev_z != 0))
+        def _():
+            signal(dev_y, dev_z)
+
+    def enter():
+        @pl.when(me_z == 0)
+        def _():
+            pl.semaphore_wait(barrier, 2)
+        @pl.when(me_z != 0)
+        def _():
+            pl.semaphore_wait(barrier, 2 + len(beside))
+        for dev_y, dev_z in beside:
+            @pl.when(jnp.logical_or(me_z == 0, dev_z == 0))
+            def _():
+                signal(dev_y, dev_z)
 
     tiles = nz // ROWS
     params = [pltpu.make_async_copy(tau_in, tau_ref, param_sem.at[0]), pltpu.make_async_copy(force_in, force_ref, param_sem.at[1])]
@@ -93,12 +112,18 @@
         rows = pl.ds(pl.multiple_of(tile * ROWS, ROWS), ROWS)
         return [pltpu.make_async_copy(field_ref.at[:, y, rows], stage.at[:, y, rows], first_sem.at[face, tile]) for face, y in enumerate((0, ny - 1))]
 
-    for position in range(tiles):
-        for copy in first_loads(position // 2 if position % 2 == 0 else tiles - 1 - position // 2):
-            copy.start()
-    loads = [pltpu.make_async_copy(field_ref.at[:, y], stage.at[:, y], load_sem.at[y]) for y in range(1, ny - 1)]
-    for copy in loads:
-        copy.start()
+    def inner_load(tile):
+        rows = pl.ds(pl.multiple_of(tile * ROWS, ROWS), ROWS)
+        planes = pl.ds(1, ny - 2)
+        return pltpu.make_async_copy(field_ref.at[:, planes, rows], stage.at[:, planes, rows], load_sem.at[tile])
+
+    order = [position // 2 if position % 2 == 0 else tiles - 1 - position // 2 for position in range(tiles)]
+    for positions in (order[:2], order[2:]):
+        for tile in positions:
+            for copy in first_loads(tile):
+                copy.start()
+        for tile in positions:
+            inner_load(tile).start()
     for copy in params:
         copy.wait()
 
@@ -233,17 +258,31 @@
         collide_faces(0, tile)
         @pl.when(position == 0)
         def _():
-            pl.semaphore_wait(barrier, len(neighbours))
-        start_faces(0, position, tile)
+            enter()
+        for copy in faces(0, tile):
+            copy.start()
 
     def first_inner(position):
-        collide_inner(0, tile_at(position))
-        start_rows(0, position)
-
-    over(0, tiles, first_faces)
-    for copy in loads:
-        copy.wait()
-    over(0, tiles, first_inner)
+        tile = tile_at(position)
+        inner_load(tile).wait()
+        collide_inner(0, tile)
+
+    def first_part(position):
+        @pl.when(jnp.logical_or(position < 2, jnp.logical_and(position >= 4, position < tiles + 2)))
+        def _():
+            first_faces(jnp.where(position < 2, position, position - 2))
+        @pl.when(jnp.logical_or(jnp.logical_and(position >= 2, position < 4), position >= tiles + 2))
+        def _():
+            first_inner(jnp.where(position < 4, position - 2, position - tiles))
+        @pl.when(position == 3)
+        def _():
+            @pl.when(me_z == 0)
+            def _():
+                pl.semaphore_wait(barrier, len(beside))
+            for copy in all_edges[0]:
+                copy.start()
+
+    over(0, 2 * tiles, first_part)
 
     for step in range(1, STEPS):
         def place(position):
@@ -328,7 +367,7 @@
                 pltpu.SMEM((1,), jnp.float32),
                 pltpu.SMEM((3,), jnp.float32),
                 pltpu.SemaphoreType.DMA((2,)),
-                pltpu.SemaphoreType.DMA((ny,)),
+                pltpu.SemaphoreType.DMA((nz // ROWS,)),
                 pltpu.SemaphoreType.DMA((2, nz // ROWS)),
                 pltpu.SemaphoreType.DMA((2, 2, nz // ROWS)),
                 pltpu.SemaphoreType.DMA((2, 2, nz // ROWS)),

time: 43.8 us -> 45.3 us (1.034)
  Pallas kernels: 42.3 us -> 43.8 us
    pallas_call x1, Pallas kernels: 37.7 us -> 39.2 us  [local_steps(): pl.pallas_call(functools.partial(step_kernel, size_y, size_z, ny, nz), na...]
where the time goes in v4:
time: 45.3 us; the launch traced here: 45.1 us
  Pallas kernels  43.8 us (97%)
  between operations  1.28 us (3%)
    pallas_call x1, Pallas kernels, local_steps(): pl.pallas_call(functools.partial(step_kernel, size_y, size_z, ny, nz), na...  39.2 us
    pallas_call x1, Pallas kernels, local_steps(): pl.pallas_call(output_kernel, name='lattice_output', out_shape=tuple((jax...  4.6 us

profile of v4, /device:TPU:0, one launch (start us, length us, event | category | flops | bytes accessed | tf_op | source)
XLA Modules:
  0.0 45.1 jit_solution(577133504055073410)
XLA Ops:
  1.3 39.2 %lattice_steps.1 = (f32[19,8,64,256]{3,2,1,0:T(8,128)S(1)}, f32[8,64,256]{2,1,0:T(8,128)S(1)}, f32[3,8,64,256]{3,2,1,0:T(8,128)S(1)}) custom-call(f32[1]{0:T(128)} %bitcast.5.tau_in, f32[3]{0:T(128)} %force_in.1, f32[19,8,64,256]{3,2,1,0:T(8,128)} %bitcast.6), custom_call_target="tpu_custom_call" | custom-call | tf_op jit(solution)/shard_map/lattice_steps/pallas_call | solution.py:354
  40.5 4.6 %lattice_output.1 = (f32[19,8,64,256]{3,2,1,0:T(8,128)}, f32[8,64,256]{2,1,0:T(8,128)}, f32[3,8,64,256]{3,2,1,0:T(8,128)}) custom-call(f32[19,8,64,256]{3,2,1,0:T(8,128)S(1)} %get-tuple-element.9.final_in, f32[8,64,256]{2,1,0:T(8,128)S(1)} %get-tuple-element.10.density_in, f32[3,8,64,256]{3,2,1,0:T(8,128)S(1)} %get-tuple-element.11.velocity_in), custom_call_target="tpu_custom_call" | custom-call | tf_op jit(solution)/shard_map/lattice_output/pallas_call | solution.py:379

commit v5 on v4

--- a/solution.py
+++ b/solution.py
@@ -117,13 +117,14 @@
         planes = pl.ds(1, ny - 2)
         return pltpu.make_async_copy(field_ref.at[:, planes, rows], stage.at[:, planes, rows], load_sem.at[tile])
 
-    order = [position // 2 if position % 2 == 0 else tiles - 1 - position // 2 for position in range(tiles)]
-    for positions in (order[:2], order[2:]):
-        for tile in positions:
-            for copy in first_loads(tile):
-                copy.start()
-        for tile in positions:
-            inner_load(tile).start()
+    def outwards(position):
+        return tiles // 2 - 1 - position // 2 if position % 2 == 0 else tiles // 2 + position // 2
+
+    for position in range(tiles):
+        for copy in first_loads(outwards(position)):
+            copy.start()
+    for position in range(tiles):
+        inner_load(outwards(tiles - 1 - position)).start()
     for copy in params:
         copy.wait()
 
@@ -213,7 +214,7 @@
                 velocity_ref[(axis, *place)] = (momentum[axis] + force[axis]) / density
 
     def tile_at(position):
-        return jnp.where(position % 2 == 0, position // 2, tiles - 1 - position // 2)
+        return jnp.where(position % 2 == 0, tiles // 2 - 1 - position // 2, tiles // 2 + position // 2)
 
     def at_position(position, number, copies):
         @pl.when(position == number)
@@ -229,27 +230,26 @@
     def collide_inner(step, tile):
         over(1, ny - 1, lambda index: collide_tile(step, index, tile), True)
 
-    def start_faces(step, position, tile):
-        at_position(position, 0, all_edges[step][0:2])
-        at_position(position, 1, all_edges[step][4:6])
+    def start_faces(step, tile):
         for copy in faces(step, tile):
             copy.start()
 
-    def start_rows(step, position):
-        at_position(position, 0, all_edges[step][2:4])
-        at_position(position, 1, all_edges[step][6:7])
+    def start_edges(step, position):
+        at_position(position, tiles - 2, all_edges[step][:4])
+        at_position(position, tiles - 1, all_edges[step][4:])
 
     def await_pieces(step, position, tile):
         def await_piece(number):
             for copy in faces(step, number):
                 copy.wait_recv()
 
-        @pl.when(position < 2)
+        @pl.when(position == 0)
         def _():
             await_piece(tile)
+            await_piece(tile + 1)
         @pl.when(position < tiles - 2)
         def _():
-            await_piece(jnp.where(position % 2 == 0, tile + 1, tile - 1))
+            await_piece(jnp.where(position % 2 == 0, tile - 1, tile + 1))
 
     def first_faces(position):
         tile = tile_at(position)
@@ -263,53 +263,55 @@
             copy.start()
 
     def first_inner(position):
-        tile = tile_at(position)
+        tile = tile_at(tiles - 1 - position)
         inner_load(tile).wait()
         collide_inner(0, tile)
-
-    def first_part(position):
-        @pl.when(jnp.logical_or(position < 2, jnp.logical_and(position >= 4, position < tiles + 2)))
-        def _():
-            first_faces(jnp.where(position < 2, position, position - 2))
-        @pl.when(jnp.logical_or(jnp.logical_and(position >= 2, position < 4), position >= tiles + 2))
-        def _():
-            first_inner(jnp.where(position < 4, position - 2, position - tiles))
-        @pl.when(position == 3)
-        def _():
-            @pl.when(me_z == 0)
-            def _():
-                pl.semaphore_wait(barrier, len(beside))
+        @pl.when(jnp.logical_and(position == 1, me_z != 0))
+        def _():
             for copy in all_edges[0]:
                 copy.start()
 
-    over(0, 2 * tiles, first_part)
+    over(0, tiles, first_faces)
+    over(0, tiles, first_inner)
+
+    @pl.when(me_z == 0)
+    def _():
+        pl.semaphore_wait(barrier, len(beside))
+        for copy in all_edges[0]:
+            copy.start()
 
     for step in range(1, STEPS):
         def place(position):
             tile = tile_at(position)
             await_pieces(step - 1, position, tile)
-            @pl.when(position == 0)
+            @pl.when(position == tiles - 2)
             def _():
                 for copy in all_edges[step - 1]:
                     copy.wait_recv()
             if step >= 2:
                 for copy in faces(step - 2, tile):
                     copy.wait_send()
-                @pl.when(position == 0)
+                @pl.when(position == tiles - 2)
                 def _():
                     for copy in all_edges[step - 2]:
                         copy.wait_send()
             collide_faces(step, tile)
-            start_faces(step, position, tile)
+            start_faces(step, tile)
             collide_inner(step, tile)
-            start_rows(step, position)
+            start_edges(step, position)
 
         over(0, tiles, place)
 
     last = STEPS - 1
-    for copy in all_edges[last]:
-        copy.wait_recv()
-    over(0, tiles, lambda tile: over(1, ny - 1, lambda y: finish_tile(y, tile)))
+    def finish_inner(position):
+        @pl.when(position == tiles - 2)
+        def _():
+            for copy in all_edges[last]:
+                copy.wait_recv()
+        tile = tile_at(position)
+        over(1, ny - 1, lambda y: finish_tile(y, tile))
+
+    over(0, tiles, finish_inner)
 
     def finish_faces(position):
         tile = tile_at(position)

time: 45.3 us -> 43.9 us (0.969)
  Pallas kernels: 43.8 us -> 42.4 us
    pallas_call x1, Pallas kernels: 39.2 us -> 37.8 us  [local_steps(): pl.pallas_call(functools.partial(step_kernel, size_y, size_z, ny, nz), na...]
where the time goes in v5:
time: 43.9 us; the launch traced here: 43.7 us
  Pallas kernels  42.4 us (97%)
  between operations  1.28 us (3%)
    pallas_call x1, Pallas kernels, local_steps(): pl.pallas_call(functools.partial(step_kernel, size_y, size_z, ny, nz), na...  37.8 us
    pallas_call x1, Pallas kernels, local_steps(): pl.pallas_call(output_kernel, name='lattice_output', out_shape=tuple((jax...  4.6 us

profile of v5, /device:TPU:0, one launch (start us, length us, event | category | flops | bytes accessed | tf_op | source)
XLA Modules:
  0.0 43.7 jit_solution(2787241828917767912)
XLA Ops:
  1.3 37.8 %lattice_steps.1 = (f32[19,8,64,256]{3,2,1,0:T(8,128)S(1)}, f32[8,64,256]{2,1,0:T(8,128)S(1)}, f32[3,8,64,256]{3,2,1,0:T(8,128)S(1)}) custom-call(f32[1]{0:T(128)} %bitcast.5.tau_in, f32[3]{0:T(128)} %force_in.1, f32[19,8,64,256]{3,2,1,0:T(8,128)} %bitcast.6), custom_call_target="tpu_custom_call" | custom-call | tf_op jit(solution)/shard_map/lattice_steps/pallas_call | solution.py:356
  39.1 4.6 %lattice_output.1 = (f32[19,8,64,256]{3,2,1,0:T(8,128)}, f32[8,64,256]{2,1,0:T(8,128)}, f32[3,8,64,256]{3,2,1,0:T(8,128)}) custom-call(f32[19,8,64,256]{3,2,1,0:T(8,128)S(1)} %get-tuple-element.9.final_in, f32[8,64,256]{2,1,0:T(8,128)S(1)} %get-tuple-element.10.density_in, f32[3,8,64,256]{3,2,1,0:T(8,128)S(1)} %get-tuple-element.11.velocity_in), custom_call_target="tpu_custom_call" | custom-call | tf_op jit(solution)/shard_map/lattice_output/pallas_call | solution.py:381

commit v6 on v4

--- a/solution.py
+++ b/solution.py
@@ -91,15 +91,10 @@
         def _():
             signal(dev_y, dev_z)
 
-    def enter():
-        @pl.when(me_z == 0)
-        def _():
-            pl.semaphore_wait(barrier, 2)
-        @pl.when(me_z != 0)
-        def _():
-            pl.semaphore_wait(barrier, 2 + len(beside))
+    def enter(count, needs_signal):
+        pl.semaphore_wait(barrier, count)
         for dev_y, dev_z in beside:
-            @pl.when(jnp.logical_or(me_z == 0, dev_z == 0))
+            @pl.when(needs_signal(dev_z))
             def _():
                 signal(dev_y, dev_z)
 
@@ -256,9 +251,9 @@
         for copy in first_loads(tile):
             copy.wait()
         collide_faces(0, tile)
-        @pl.when(position == 0)
-        def _():
-            enter()
+        @pl.when(jnp.logical_and(position == 0, me_z != 0))
+        def _():
+            enter(2 + len(beside), lambda dev_z: dev_z == 0)
         for copy in faces(0, tile):
             copy.start()
 
@@ -267,22 +262,35 @@
         inner_load(tile).wait()
         collide_inner(0, tile)
 
-    def first_part(position):
-        @pl.when(jnp.logical_or(position < 2, jnp.logical_and(position >= 4, position < tiles + 2)))
-        def _():
-            first_faces(jnp.where(position < 2, position, position - 2))
-        @pl.when(jnp.logical_or(jnp.logical_and(position >= 2, position < 4), position >= tiles + 2))
-        def _():
-            first_inner(jnp.where(position < 4, position - 2, position - tiles))
-        @pl.when(position == 3)
-        def _():
-            @pl.when(me_z == 0)
-            def _():
-                pl.semaphore_wait(barrier, len(beside))
+    split = jnp.where(me_z == 0, tiles, 2)
+
+    def first_part(number):
+        early = number < 2 * split
+        local = jnp.where(early, number, number - 2 * split)
+        length = jnp.where(early, split, tiles - split)
+        position = jnp.where(early, 0, split) + jnp.where(local < length, local, local - length)
+        @pl.when(local < length)
+        def _():
+            first_faces(position)
+        @pl.when(local >= length)
+        def _():
+            first_inner(position)
+        @pl.when(jnp.logical_and(number == 3, me_z != 0))
+        def _():
             for copy in all_edges[0]:
                 copy.start()
 
+    @pl.when(me_z == 0)
+    def _():
+        enter(2, lambda dev_z: dev_z != me_z)
+
     over(0, 2 * tiles, first_part)
+
+    @pl.when(me_z == 0)
+    def _():
+        pl.semaphore_wait(barrier, len(beside))
+        for copy in all_edges[0]:
+            copy.start()
 
     for step in range(1, STEPS):
         def place(position):
@@ -307,9 +315,15 @@
         over(0, tiles, place)
 
     last = STEPS - 1
-    for copy in all_edges[last]:
-        copy.wait_recv()
-    over(0, tiles, lambda tile: over(1, ny - 1, lambda y: finish_tile(y, tile)))
+    def finish_inner(position):
+        @pl.when(position == tiles - 2)
+        def _():
+            for copy in all_edges[last]:
+                copy.wait_recv()
+        tile = tile_at(tiles - 1 - position)
+        over(1, ny - 1, lambda y: finish_tile(y, tile))
+
+    over(0, tiles, finish_inner)
 
     def finish_faces(position):
         tile = tile_at(position)

time: 45.3 us -> 43 us (0.949)
  Pallas kernels: 43.8 us -> 41.5 us
    pallas_call x1, Pallas kernels: 39.2 us -> 36.9 us  [local_steps(): pl.pallas_call(functools.partial(step_kernel, size_y, size_z, ny, nz), na...]
where the time goes in v6:
time: 43 us; the launch traced here: 42.8 us
  Pallas kernels  41.5 us (97%)
  between operations  1.28 us (3%)
    pallas_call x1, Pallas kernels, local_steps(): pl.pallas_call(functools.partial(step_kernel, size_y, size_z, ny, nz), na...  36.9 us
    pallas_call x1, Pallas kernels, local_steps(): pl.pallas_call(output_kernel, name='lattice_output', out_shape=tuple((jax...  4.6 us

profile of v6, /device:TPU:0, one launch (start us, length us, event | category | flops | bytes accessed | tf_op | source)
XLA Modules:
  0.0 42.8 jit_solution(15383973948100202852)
XLA Ops:
  1.3 36.9 %lattice_steps.1 = (f32[19,8,64,256]{3,2,1,0:T(8,128)S(1)}, f32[8,64,256]{2,1,0:T(8,128)S(1)}, f32[3,8,64,256]{3,2,1,0:T(8,128)S(1)}) custom-call(f32[1]{0:T(128)} %bitcast.5.tau_in, f32[3]{0:T(128)} %force_in.1, f32[19,8,64,256]{3,2,1,0:T(8,128)} %bitcast.6), custom_call_target="tpu_custom_call" | custom-call | tf_op jit(solution)/shard_map/lattice_steps/pallas_call | solution.py:368
  38.2 4.6 %lattice_output.1 = (f32[19,8,64,256]{3,2,1,0:T(8,128)}, f32[8,64,256]{2,1,0:T(8,128)}, f32[3,8,64,256]{3,2,1,0:T(8,128)}) custom-call(f32[19,8,64,256]{3,2,1,0:T(8,128)S(1)} %get-tuple-element.9.final_in, f32[8,64,256]{2,1,0:T(8,128)S(1)} %get-tuple-element.10.density_in, f32[3,8,64,256]{3,2,1,0:T(8,128)S(1)} %get-tuple-element.11.velocity_in), custom_call_target="tpu_custom_call" | custom-call | tf_op jit(solution)/shard_map/lattice_output/pallas_call | solution.py:393

commit v7 on v6

--- a/solution.py
+++ b/solution.py
@@ -254,6 +254,11 @@
         @pl.when(jnp.logical_and(position == 0, me_z != 0))
         def _():
             enter(2 + len(beside), lambda dev_z: dev_z == 0)
+        for number, corners in enumerate((all_edges[0][0:2], all_edges[0][4:6])):
+            @pl.when(jnp.logical_and(position == number, me_z != 0))
+            def _():
+                for copy in corners:
+                    copy.start()
         for copy in faces(0, tile):
             copy.start()
 
@@ -262,7 +267,7 @@
         inner_load(tile).wait()
         collide_inner(0, tile)
 
-    split = jnp.where(me_z == 0, tiles, 2)
+    split = jnp.where(me_z == 0, tiles // 2, 2)
 
     def first_part(number):
         early = number < 2 * split
@@ -275,9 +280,14 @@
         @pl.when(local >= length)
         def _():
             first_inner(position)
-        @pl.when(jnp.logical_and(number == 3, me_z != 0))
-        def _():
-            for copy in all_edges[0]:
+        @pl.when(number == 2 * split - 1)
+        def _():
+            @pl.when(me_z == 0)
+            def _():
+                pl.semaphore_wait(barrier, len(beside))
+                for copy in all_edges[0][0:2] + all_edges[0][4:6]:
+                    copy.start()
+            for copy in all_edges[0][2:4] + all_edges[0][6:7]:
                 copy.start()
 
     @pl.when(me_z == 0)
@@ -285,12 +295,6 @@
         enter(2, lambda dev_z: dev_z != me_z)
 
     over(0, 2 * tiles, first_part)
-
-    @pl.when(me_z == 0)
-    def _():
-        pl.semaphore_wait(barrier, len(beside))
-        for copy in all_edges[0]:
-            copy.start()
 
     for step in range(1, STEPS):
         def place(position):

time: 43 us -> 42.9 us (level)
  no operation moved by 1% of the time
where the time goes in v7:
time: 42.9 us; the launch traced here: 42.7 us
  Pallas kernels  41.4 us (97%)
  between operations  1.28 us (3%)
    pallas_call x1, Pallas kernels, local_steps(): pl.pallas_call(functools.partial(step_kernel, size_y, size_z, ny, nz), na...  36.8 us
    pallas_call x1, Pallas kernels, local_steps(): pl.pallas_call(output_kernel, name='lattice_output', out_shape=tuple((jax...  4.6 us

profile of v7, /device:TPU:0, one launch (start us, length us, event | category | flops | bytes accessed | tf_op | source)
XLA Modules:
  0.0 42.7 jit_solution(17898589916682866136)
XLA Ops:
  1.3 36.8 %lattice_steps.1 = (f32[19,8,64,256]{3,2,1,0:T(8,128)S(1)}, f32[8,64,256]{2,1,0:T(8,128)S(1)}, f32[3,8,64,256]{3,2,1,0:T(8,128)S(1)}) custom-call(f32[1]{0:T(128)} %bitcast.5.tau_in, f32[3]{0:T(128)} %force_in.1, f32[19,8,64,256]{3,2,1,0:T(8,128)} %bitcast.6), custom_call_target="tpu_custom_call" | custom-call | tf_op jit(solution)/shard_map/lattice_steps/pallas_call | solution.py:372
  38.1 4.6 %lattice_output.1 = (f32[19,8,64,256]{3,2,1,0:T(8,128)}, f32[8,64,256]{2,1,0:T(8,128)}, f32[3,8,64,256]{3,2,1,0:T(8,128)}) custom-call(f32[19,8,64,256]{3,2,1,0:T(8,128)S(1)} %get-tuple-element.9.final_in, f32[8,64,256]{2,1,0:T(8,128)S(1)} %get-tuple-element.10.density_in, f32[3,8,64,256]{3,2,1,0:T(8,128)S(1)} %get-tuple-element.11.velocity_in), custom_call_target="tpu_custom_call" | custom-call | tf_op jit(solution)/shard_map/lattice_output/pallas_call | solution.py:397

commit v8 on v7

--- a/solution.py
+++ b/solution.py
@@ -91,12 +91,10 @@
         def _():
             signal(dev_y, dev_z)
 
-    def enter(count, needs_signal):
+    def enter(count, targets):
         pl.semaphore_wait(barrier, count)
-        for dev_y, dev_z in beside:
-            @pl.when(needs_signal(dev_z))
-            def _():
-                signal(dev_y, dev_z)
+        for dev_z in targets:
+            signal(me_y, dev_z)
 
     tiles = nz // ROWS
     params = [pltpu.make_async_copy(tau_in, tau_ref, param_sem.at[0]), pltpu.make_async_copy(force_in, force_ref, param_sem.at[1])]
@@ -251,9 +249,17 @@
         for copy in first_loads(tile):
             copy.wait()
         collide_faces(0, tile)
-        @pl.when(jnp.logical_and(position == 0, me_z != 0))
-        def _():
-            enter(2 + len(beside), lambda dev_z: dev_z == 0)
+        @pl.when(position == 0)
+        def _():
+            @pl.when(jnp.logical_and(me_z != 0, jnp.logical_and(down_z != 0, up_z != 0)))
+            def _():
+                enter(8, ())
+            @pl.when(jnp.logical_and(me_z != 0, down_z == 0))
+            def _():
+                enter(6, (down_z,))
+            @pl.when(jnp.logical_and(me_z != 0, up_z == 0))
+            def _():
+                enter(6, (up_z,))
         for number, corners in enumerate((all_edges[0][0:2], all_edges[0][4:6])):
             @pl.when(jnp.logical_and(position == number, me_z != 0))
             def _():
@@ -284,7 +290,7 @@
         def _():
             @pl.when(me_z == 0)
             def _():
-                pl.semaphore_wait(barrier, len(beside))
+                pl.semaphore_wait(barrier, 2)
                 for copy in all_edges[0][0:2] + all_edges[0][4:6]:
                     copy.start()
             for copy in all_edges[0][2:4] + all_edges[0][6:7]:
@@ -292,7 +298,7 @@
 
     @pl.when(me_z == 0)
     def _():
-        enter(2, lambda dev_z: dev_z != me_z)
+        enter(2, (down_z, up_z))
 
     over(0, 2 * tiles, first_part)
 

time: 42.9 us -> 40.8 us (0.951)
  Pallas kernels: 41.4 us -> 39.4 us
    pallas_call x1, Pallas kernels: 36.8 us -> 34.8 us  [local_steps(): pl.pallas_call(functools.partial(step_kernel, size_y, size_z, ny, nz), na...]
where the time goes in v8:
time: 40.8 us; the launch traced here: 40.7 us
  Pallas kernels  39.4 us (97%)
  between operations  1.28 us (3%)
    pallas_call x1, Pallas kernels, local_steps(): pl.pallas_call(functools.partial(step_kernel, size_y, size_z, ny, nz), na...  34.8 us
    pallas_call x1, Pallas kernels, local_steps(): pl.pallas_call(output_kernel, name='lattice_output', out_shape=tuple((jax...  4.6 us

profile of v8, /device:TPU:0, one launch (start us, length us, event | category | flops | bytes accessed | tf_op | source)
XLA Modules:
  0.0 40.7 jit_solution(5170875384687697053)
XLA Ops:
  1.3 34.8 %lattice_steps.1 = (f32[19,8,64,256]{3,2,1,0:T(8,128)S(1)}, f32[8,64,256]{2,1,0:T(8,128)S(1)}, f32[3,8,64,256]{3,2,1,0:T(8,128)S(1)}) custom-call(f32[1]{0:T(128)} %bitcast.5.tau_in, f32[3]{0:T(128)} %force_in.1, f32[19,8,64,256]{3,2,1,0:T(8,128)} %bitcast.6), custom_call_target="tpu_custom_call" | custom-call | tf_op jit(solution)/shard_map/lattice_steps/pallas_call | solution.py:378
  36.1 4.6 %lattice_output.1 = (f32[19,8,64,256]{3,2,1,0:T(8,128)}, f32[8,64,256]{2,1,0:T(8,128)}, f32[3,8,64,256]{3,2,1,0:T(8,128)}) custom-call(f32[19,8,64,256]{3,2,1,0:T(8,128)S(1)} %get-tuple-element.9.final_in, f32[8,64,256]{2,1,0:T(8,128)S(1)} %get-tuple-element.10.density_in, f32[3,8,64,256]{3,2,1,0:T(8,128)S(1)} %get-tuple-element.11.velocity_in), custom_call_target="tpu_custom_call" | custom-call | tf_op jit(solution)/shard_map/lattice_output/pallas_call | solution.py:403

commit v9 on v7

--- a/solution.py
+++ b/solution.py
@@ -79,24 +79,19 @@
         return {"py": dev_y, "pz": dev_z}
 
     barrier = pltpu.get_barrier_semaphore()
-    beside = [(dev_y, dev_z) for dev_z in (down_z, up_z) for dev_y in (down_y, me_y, up_y)]
+    even = me_z % 2 == 0
+    odd = me_z % 2 == 1
 
     def signal(dev_y, dev_z):
         pl.semaphore_signal(barrier, inc=1, device_id=device(dev_y, dev_z), device_id_type=MESH)
 
     signal(up_y, me_z)
     signal(down_y, me_z)
-    for dev_y, dev_z in beside:
-        @pl.when(jnp.logical_and(me_z != 0, dev_z != 0))
-        def _():
-            signal(dev_y, dev_z)
-
-    def enter(count, needs_signal):
+
+    def enter(count):
         pl.semaphore_wait(barrier, count)
-        for dev_y, dev_z in beside:
-            @pl.when(needs_signal(dev_z))
-            def _():
-                signal(dev_y, dev_z)
+        signal(me_y, down_z)
+        signal(me_y, up_z)
 
     tiles = nz // ROWS
     params = [pltpu.make_async_copy(tau_in, tau_ref, param_sem.at[0]), pltpu.make_async_copy(force_in, force_ref, param_sem.at[1])]
@@ -251,11 +246,11 @@
         for copy in first_loads(tile):
             copy.wait()
         collide_faces(0, tile)
-        @pl.when(jnp.logical_and(position == 0, me_z != 0))
-        def _():
-            enter(2 + len(beside), lambda dev_z: dev_z == 0)
+        @pl.when(jnp.logical_and(position == 0, odd))
+        def _():
+            enter(4)
         for number, corners in enumerate((all_edges[0][0:2], all_edges[0][4:6])):
-            @pl.when(jnp.logical_and(position == number, me_z != 0))
+            @pl.when(jnp.logical_and(position == number, odd))
             def _():
                 for copy in corners:
                     copy.start()
@@ -267,7 +262,7 @@
         inner_load(tile).wait()
         collide_inner(0, tile)
 
-    split = jnp.where(me_z == 0, tiles // 2, 2)
+    split = jnp.where(even, tiles // 2, 2)
 
     def first_part(number):
         early = number < 2 * split
@@ -282,17 +277,17 @@
             first_inner(position)
         @pl.when(number == 2 * split - 1)
         def _():
-            @pl.when(me_z == 0)
+            @pl.when(even)
             def _():
-                pl.semaphore_wait(barrier, len(beside))
+                pl.semaphore_wait(barrier, 2)
                 for copy in all_edges[0][0:2] + all_edges[0][4:6]:
                     copy.start()
             for copy in all_edges[0][2:4] + all_edges[0][6:7]:
                 copy.start()
 
-    @pl.when(me_z == 0)
+    @pl.when(even)
     def _():
-        enter(2, lambda dev_z: dev_z != me_z)
+        enter(2)
 
     over(0, 2 * tiles, first_part)
 

time: 42.9 us -> 41.1 us (0.958)
  Pallas kernels: 41.4 us -> 39.6 us
    pallas_call x1, Pallas kernels: 36.8 us -> 35 us  [local_steps(): pl.pallas_call(functools.partial(step_kernel, size_y, size_z, ny, nz), na...]
where the time goes in v9:
time: 41.1 us; the launch traced here: 40.9 us
  Pallas kernels  39.6 us (96%)
  between operations  1.28 us (3%)
    pallas_call x1, Pallas kernels, local_steps(): pl.pallas_call(functools.partial(step_kernel, size_y, size_z, ny, nz), na...  35 us
    pallas_call x1, Pallas kernels, local_steps(): pl.pallas_call(output_kernel, name='lattice_output', out_shape=tuple((jax...  4.6 us

profile of v9, /device:TPU:0, one launch (start us, length us, event | category | flops | bytes accessed | tf_op | source)
XLA Modules:
  0.0 40.9 jit_solution(12123260932304385438)
XLA Ops:
  1.3 35.0 %lattice_steps.1 = (f32[19,8,64,256]{3,2,1,0:T(8,128)S(1)}, f32[8,64,256]{2,1,0:T(8,128)S(1)}, f32[3,8,64,256]{3,2,1,0:T(8,128)S(1)}) custom-call(f32[1]{0:T(128)} %bitcast.5.tau_in, f32[3]{0:T(128)} %force_in.1, f32[19,8,64,256]{3,2,1,0:T(8,128)} %bitcast.6), custom_call_target="tpu_custom_call" | custom-call | tf_op jit(solution)/shard_map/lattice_steps/pallas_call | solution.py:367
  36.3 4.6 %lattice_output.1 = (f32[19,8,64,256]{3,2,1,0:T(8,128)}, f32[8,64,256]{2,1,0:T(8,128)}, f32[3,8,64,256]{3,2,1,0:T(8,128)}) custom-call(f32[19,8,64,256]{3,2,1,0:T(8,128)S(1)} %get-tuple-element.9.final_in, f32[8,64,256]{2,1,0:T(8,128)S(1)} %get-tuple-element.10.density_in, f32[3,8,64,256]{3,2,1,0:T(8,128)S(1)} %get-tuple-element.11.velocity_in), custom_call_target="tpu_custom_call" | custom-call | tf_op jit(solution)/shard_map/lattice_output/pallas_call | solution.py:392

commit v10 on v8

--- a/solution.py
+++ b/solution.py
@@ -353,12 +353,16 @@
             copy.wait_send()
 
 
-def output_kernel(final_in, density_in, velocity_in, final_ref, density_ref, velocity_ref, final_sem, moment_sem):
-    copies = [pltpu.make_async_copy(final_in.at[pop_id], final_ref.at[pop_id], final_sem.at[pop_id]) for pop_id in range(19)]
-    copies.append(pltpu.make_async_copy(density_in, density_ref, moment_sem.at[0]))
-    copies.append(pltpu.make_async_copy(velocity_in, velocity_ref, moment_sem.at[1]))
-    for copy in copies:
-        copy.start()
+def output_kernel(final_in, density_in, velocity_in, final_ref, density_ref, velocity_ref, copy_sem):
+    copies = []
+    for first in range(0, final_in.shape[1], 2):
+        planes = pl.ds(first, 2)
+        pairs = [(final_in.at[pop_id, planes], final_ref.at[pop_id, planes]) for pop_id in range(19)]
+        pairs += [(velocity_in.at[axis, planes], velocity_ref.at[axis, planes]) for axis in range(3)]
+        pairs.append((density_in.at[planes], density_ref.at[planes]))
+        for source, target in pairs:
+            copies.append(pltpu.make_async_copy(source, target, copy_sem.at[len(copies)]))
+            copies[-1].start()
     for copy in copies:
         copy.wait()
 
@@ -406,7 +410,7 @@
             out_shape=tuple(jax.ShapeDtypeStruct(result.shape, result.dtype) for result in results),
             in_specs=[vmem, vmem, vmem],
             out_specs=(anywhere, anywhere, anywhere),
-            scratch_shapes=[pltpu.SemaphoreType.DMA((19,)), pltpu.SemaphoreType.DMA((2,))],
+            scratch_shapes=[pltpu.SemaphoreType.DMA((23 * ny // 2,))],
             compiler_params=pltpu.CompilerParams(vmem_limit_bytes=2**20),
         )(*results)
         return jnp.transpose(final, (0, 3, 1, 2)), jnp.transpose(density, (2, 0, 1)), jnp.transpose(velocity, (0, 3, 1, 2))

time: 40.8 us -> 41.4 us (1.015)
  Pallas kernels: 39.4 us -> 39.9 us
    pallas_call x1, Pallas kernels: 4.6 us -> 5.14 us  [local_steps(): pl.pallas_call(output_kernel, name='lattice_output', out_shape=tuple((jax...]
where the time goes in v10:
time: 41.4 us; the launch traced here: 41.2 us
  Pallas kernels  39.9 us (96%)
  between operations  1.28 us (3%)
    pallas_call x1, Pallas kernels, local_steps(): pl.pallas_call(functools.partial(step_kernel, size_y, size_z, ny, nz), na...  34.8 us
    pallas_call x1, Pallas kernels, local_steps(): pl.pallas_call(output_kernel, name='lattice_output', out_shape=tuple((jax...  5.14 us

profile of v10, /device:TPU:0, one launch (start us, length us, event | category | flops | bytes accessed | tf_op | source)
XLA Modules:
  0.0 41.2 jit_solution(8896162156346176463)
XLA Ops:
  1.3 34.8 %lattice_steps.1 = (f32[19,8,64,256]{3,2,1,0:T(8,128)S(1)}, f32[8,64,256]{2,1,0:T(8,128)S(1)}, f32[3,8,64,256]{3,2,1,0:T(8,128)S(1)}) custom-call(f32[1]{0:T(128)} %bitcast.5.tau_in, f32[3]{0:T(128)} %force_in.1, f32[19,8,64,256]{3,2,1,0:T(8,128)} %bitcast.6), custom_call_target="tpu_custom_call" | custom-call | tf_op jit(solution)/shard_map/lattice_steps/pallas_call | solution.py:382
  36.1 5.1 %lattice_output.1 = (f32[19,8,64,256]{3,2,1,0:T(8,128)}, f32[8,64,256]{2,1,0:T(8,128)}, f32[3,8,64,256]{3,2,1,0:T(8,128)}) custom-call(f32[19,8,64,256]{3,2,1,0:T(8,128)S(1)} %get-tuple-element.9.final_in, f32[8,64,256]{2,1,0:T(8,128)S(1)} %get-tuple-element.10.density_in, f32[3,8,64,256]{3,2,1,0:T(8,128)S(1)} %get-tuple-element.11.velocity_in), custom_call_target="tpu_custom_call" | custom-call | tf_op jit(solution)/shard_map/lattice_output/pallas_call | solution.py:407

commit v11 on v8

--- a/solution.py
+++ b/solution.py
@@ -353,10 +353,10 @@
             copy.wait_send()
 
 
-def output_kernel(final_in, density_in, velocity_in, final_ref, density_ref, velocity_ref, final_sem, moment_sem):
-    copies = [pltpu.make_async_copy(final_in.at[pop_id], final_ref.at[pop_id], final_sem.at[pop_id]) for pop_id in range(19)]
-    copies.append(pltpu.make_async_copy(density_in, density_ref, moment_sem.at[0]))
-    copies.append(pltpu.make_async_copy(velocity_in, velocity_ref, moment_sem.at[1]))
+def output_kernel(final_in, density_in, velocity_in, final_ref, density_ref, velocity_ref, copy_sem):
+    pairs = [(final_in.at[pl.ds(first, count)], final_ref.at[pl.ds(first, count)]) for first, count in ((0, 4), (4, 4), (8, 4), (12, 4), (16, 3))]
+    pairs += [(velocity_in, velocity_ref), (density_in, density_ref)]
+    copies = [pltpu.make_async_copy(source, target, copy_sem.at[number]) for number, (source, target) in enumerate(pairs)]
     for copy in copies:
         copy.start()
     for copy in copies:
@@ -406,7 +406,7 @@
             out_shape=tuple(jax.ShapeDtypeStruct(result.shape, result.dtype) for result in results),
             in_specs=[vmem, vmem, vmem],
             out_specs=(anywhere, anywhere, anywhere),
-            scratch_shapes=[pltpu.SemaphoreType.DMA((19,)), pltpu.SemaphoreType.DMA((2,))],
+            scratch_shapes=[pltpu.SemaphoreType.DMA((7,))],
             compiler_params=pltpu.CompilerParams(vmem_limit_bytes=2**20),
         )(*results)
         return jnp.transpose(final, (0, 3, 1, 2)), jnp.transpose(density, (2, 0, 1)), jnp.transpose(velocity, (0, 3, 1, 2))

time: 40.8 us -> 40.7 us (level)
  no operation moved by 1% of the time
where the time goes in v11:
time: 40.7 us; the launch traced here: 40.5 us
  Pallas kernels  39.2 us (96%)
  between operations  1.28 us (3%)
    pallas_call x1, Pallas kernels, local_steps(): pl.pallas_call(functools.partial(step_kernel, size_y, size_z, ny, nz), na...  34.8 us
    pallas_call x1, Pallas kernels, local_steps(): pl.pallas_call(output_kernel, name='lattice_output', out_shape=tuple((jax...  4.44 us

profile of v11, /device:TPU:0, one launch (start us, length us, event | category | flops | bytes accessed | tf_op | source)
XLA Modules:
  0.0 40.5 jit_solution(18049481499038280708)
XLA Ops:
  1.3 34.8 %lattice_steps.1 = (f32[19,8,64,256]{3,2,1,0:T(8,128)S(1)}, f32[8,64,256]{2,1,0:T(8,128)S(1)}, f32[3,8,64,256]{3,2,1,0:T(8,128)S(1)}) custom-call(f32[1]{0:T(128)} %bitcast.5.tau_in, f32[3]{0:T(128)} %force_in.1, f32[19,8,64,256]{3,2,1,0:T(8,128)} %bitcast.6), custom_call_target="tpu_custom_call" | custom-call | tf_op jit(solution)/shard_map/lattice_steps/pallas_call | solution.py:378
  36.1 4.4 %lattice_output.1 = (f32[19,8,64,256]{3,2,1,0:T(8,128)}, f32[8,64,256]{2,1,0:T(8,128)}, f32[3,8,64,256]{3,2,1,0:T(8,128)}) custom-call(f32[19,8,64,256]{3,2,1,0:T(8,128)S(1)} %get-tuple-element.9.final_in, f32[8,64,256]{2,1,0:T(8,128)S(1)} %get-tuple-element.10.density_in, f32[3,8,64,256]{3,2,1,0:T(8,128)S(1)} %get-tuple-element.11.velocity_in), custom_call_target="tpu_custom_call" | custom-call | tf_op jit(solution)/shard_map/lattice_output/pallas_call | solution.py:403
